TPU v7x, 32 devices: a whole 2x2x4 slice. The times are simulated.
32 devices in a mesh: gx: 4 (over y, x), gy: 4 (over z), gz: 2 (over core).
Axes of the slice: x: 2, y: 2, z: 4, core: 2. Of those that a mesh axis runs over, the one named last changes fastest.
Arguments:
- old_data: float32 [384, 5, 16, 256], P(('gx', 'gy', 'gz')), may hold values from -6 to 24, as said below
- pair_old: int32 [256], P(('gx', 'gy', 'gz')), may hold values from 0 to 11
- pair_slot: int32 [256], P(('gx', 'gy', 'gz')), may hold values from 0 to 2
- pair_shift: int32 [256, 3], P(('gx', 'gy', 'gz')), may hold values from -2 to 2
- pair_dest: int32 [256, 1], P(('gx', 'gy', 'gz')), may hold values from 0 to 7; in each aligned block of 8 rows (0 to 7, 8 to 15, ...) at most 2 rows name the same one
- new_ratio: int32 [96], replicated, may hold values from 1 to 2, as said below
- neighbor_side: int32 [96, 6], P(('gx', 'gy', 'gz')), may hold values from 0 to 3
- neighbor_patch: int32 [96, 6], P(('gx', 'gy', 'gz')), may hold values from 0 to 2
Outputs:
- new_data: float32 [96, 5, 16, 256], P(('gx', 'gy', 'gz'))
- interface_jump: float32 [96, 5, 6, 256], P(('gx', 'gy', 'gz'))
- mass_totals: float32 [2, 5], replicated
Inputs may be any that keep to these rules, and one draw needn't show every extreme that they name: `old_data`: values of order one whose level differs from patch to patch and field to field. `pair_dest`: on the rows of one device no owner is named more than 2 times, and some device names some owner exactly 2 times. `new_ratio`: 1 marks a new patch on the old level, 2 one coarser by a factor of two in each direction. `neighbor_side`: 0: on the device before in the order d, 1: on the same device, 2: on the device after, 3: no neighbour.
All inputs are finite; a program needn't handle non-finite values.
Results may differ from a plain program's by a relative error of at most 0.0001.
Values sent between devices are 32-bit elements; how exact they have to be, the bound alone decides.
A program may use at most 64 MiB of HBM per device.

v0:
```python
import functools

import jax
import jax.numpy as jnp
from jax import lax
from jax.experimental import pallas as pl
from jax.experimental.pallas import tpu as pltpu
from jax.sharding import PartitionSpec as P

MESH = pl.DeviceIdType.MESH
AXES = ("gx", "gy", "gz")


def split_two(value):
    high = value.astype(jnp.bfloat16)
    low = (value - high.astype(jnp.float32)).astype(jnp.bfloat16)
    return high, low


def dot(a, b):
    return jnp.dot(a, b, preferred_element_type=jnp.float32)


def iota(shape, axis):
    return lax.broadcasted_iota(jnp.int32, shape, axis)


def kernel(
    dims,
    old_hbm,
    pair_old_hbm,
    pair_slot_hbm,
    pair_shift_hbm,
    pair_dest_hbm,
    new_ratio_hbm,
    side_hbm,
    patch_hbm,
    new_out,
    jump_out,
    mass_out,
    pair_old,
    pair_slot,
    pair_shift,
    pair_dest,
    new_ratio,
    side_ref,
    patch_ref,
    old,
    parts,
    mine,
    theirs,
    partner_in,
    chip_in,
    spread,
    faces,
    ghosts,
    mass_group,
    mass_line,
    old_sem,
    table_sem,
    turn,
    d2d_send,
    d2d_recv,
    chip_send,
    chip_recv,
    face_send,
    face_recv,
    group_send,
    group_recv,
    line_send,
    line_recv,
):
    size_x, size_y, size_z, n_old, n_new, n_pairs, fields, edge = dims
    face = edge * edge
    rows = fields * edge
    half = edge // 2
    group = size_x * size_z
    chips = group // 2
    bits = chips.bit_length() - 1
    devices = group * size_y
    ix, iy, iz = (lax.axis_index(a) for a in AXES)
    rank = ix * size_z + iz
    core = lax.rem(rank, 2)
    chip = lax.div(rank, 2)
    linear = (ix * size_y + iy) * size_z + iz

    def at_rank(g):
        return (lax.div(g, size_z), iy, lax.rem(g, size_z))

    def at_linear(d):
        return (
            lax.div(d, size_y * size_z),
            lax.rem(lax.div(d, size_z), size_y),
            lax.rem(d, size_z),
        )

    def chip_at(x):
        other = chip
        for b in range(bits):
            if (x >> b) & 1:
                other = other + (1 - 2 * lax.rem(lax.div(chip, 1 << b), 2)) * (1 << b)
        return other

    has_before = linear > 0
    has_after = linear < devices - 1
    partner = at_rank(chip * 2 + 1 - core)

    old_copy = pltpu.make_async_copy(old_hbm, old, old_sem)
    old_copy.start()
    tables = (
        (pair_dest_hbm, pair_dest),
        (pair_slot_hbm, pair_slot),
        (new_ratio_hbm, new_ratio),
        (pair_old_hbm, pair_old),
        (pair_shift_hbm, pair_shift),
        (side_hbm, side_ref),
        (patch_hbm, patch_ref),
    )
    tables = [
        pltpu.make_async_copy(source, table, table_sem.at[i])
        for i, (source, table) in enumerate(tables)
    ]
    for table in tables:
        table.start()

    barrier = pltpu.get_barrier_semaphore()
    for k in range(1, group):
        pl.semaphore_signal(
            barrier, inc=1, device_id=at_rank(lax.rem(rank + k, group)), device_id_type=MESH
        )
    for k in range(1, size_y):
        pl.semaphore_signal(
            barrier, inc=1, device_id=(ix, lax.rem(iy + k, size_y), iz), device_id_type=MESH
        )

    @pl.when(has_before)
    def _():
        pl.semaphore_signal(barrier, inc=1, device_id=at_linear(linear - 1), device_id_type=MESH)

    @pl.when(has_after)
    def _():
        pl.semaphore_signal(barrier, inc=1, device_id=at_linear(linear + 1), device_id_type=MESH)

    col = iota((face, face), 1)
    row = iota((face, face), 0)
    low_col = lax.rem(col, edge)
    for i, wanted in enumerate(
        (low_col, low_col + face - edge, low_col * edge, low_col * edge + edge - 1)
    ):
        spread[:, i * face : (i + 1) * face] = jnp.where(row == wanted, 1.0, 0.0).astype(
            jnp.bfloat16
        )

    @pl.when(jnp.logical_not(has_before))
    def _():
        ghosts[0:n_new] = jnp.zeros((n_new, *ghosts.shape[1:]), jnp.float32)

    @pl.when(jnp.logical_not(has_after))
    def _():
        ghosts[2 * n_new :] = jnp.zeros((n_new, *ghosts.shape[1:]), jnp.float32)

    for table in tables:
        table.wait()
    keys, ratios = [], []
    for p in range(n_pairs):
        target = pair_dest[p]
        owner = (lax.div(target, size_z) * size_y + iy) * size_z + lax.rem(target, size_z)
        keys.append(target * n_new + pair_slot[p])
        ratios.append(new_ratio[owner * n_new + pair_slot[p]])

    parts[n_pairs] = jnp.zeros(parts.shape[1:], jnp.float32)
    row_y = lax.div(row, edge)
    row_z = lax.rem(row, edge)
    l_row = iota((rows, 2 * rows), 0)
    l_col = iota((rows, 2 * rows), 1)
    l_col = jnp.where(l_col >= rows, l_col - rows, l_col)
    same_field = lax.div(l_row, edge) == lax.div(l_col, edge)
    l_i = lax.rem(l_row, edge)
    l_m = lax.rem(l_col, edge)

    old_copy.wait()

    old_acc = [jnp.zeros((8, face), jnp.float32) for _ in range(fields)]
    for o in range(n_old):
        for f in range(fields):
            for h in range(edge // 8):
                old_acc[f] = old_acc[f] + old[o, f, h * 8 : (h + 1) * 8, :]

    new_acc = [jnp.zeros((8, face), jnp.float32) for _ in range(fields)]
    for p in range(n_pairs):
        ratio = ratios[p]
        coarse = ratio == 2
        step = ratio - 1
        tx, ty, tz = pair_shift[0, p], pair_shift[1, p], pair_shift[2, p]
        scale = jnp.where(coarse, jnp.float32(0.125), jnp.float32(1.0))
        cube = jnp.where(coarse, jnp.float32(8.0), jnp.float32(1.0))
        block = old[pair_old[p]].reshape(rows, face)
        lx = (lax.shift_right_arithmetic(l_m - tx, jnp.full_like(l_m, step)) == l_i) & same_field
        lx = jnp.where(lx, 1.0, 0.0).astype(jnp.bfloat16)
        high, low = split_two(block)
        mixed = dot(lx, jnp.concatenate([high, low], axis=0))
        ky = lax.shift_right_arithmetic(row_y - ty, jnp.full_like(row, step))
        kz = lax.shift_right_arithmetic(row_z - tz, jnp.full_like(row, step))
        code = jnp.where((kz >= 0) & (kz < edge), ky * edge + kz, -1)
        weight = jnp.where(code == col, scale, jnp.float32(0.0)).astype(jnp.bfloat16)
        high, low = split_two(mixed)
        out = dot(high, weight) + dot(low, weight)
        for f in range(fields):
            for c in range(2):
                piece = out[f * edge + c * half : f * edge + (c + 1) * half]
                parts[p, c, f] = piece
                new_acc[f] = new_acc[f] + cube * piece

    zero_rows = jnp.zeros((8 - fields, 128), jnp.float32)

    def lines(accs):
        out = [
            jnp.sum(a[:, :128] + a[:, 128:], axis=0, keepdims=True) for a in accs
        ]
        return jnp.concatenate(out + [zero_rows], axis=0)

    mass_group[0, 0:8] = lines(old_acc)
    mass_group[0, 8:16] = lines(new_acc)

    def owner_sum(dst, x, core_of):
        target = chip_at(x) * 2 + core_of
        for s in range(n_new):
            wanted = target * n_new + s
            first = jnp.int32(n_pairs)
            second = jnp.int32(n_pairs)
            for p in reversed(range(n_pairs)):
                hit = keys[p] == wanted
                second = jnp.where(hit, first, second)
                first = jnp.where(hit, jnp.int32(p), first)
            dst[x, :, s] = parts[first] + parts[second]

    orders = [list(range(bits)), list(reversed(range(bits)))]

    def sends(order, j):
        done = sum(1 << b for b in order[:j])
        xs = [x for x in range(chips) if (x >> order[j]) & 1 and not x & done]
        return sorted(xs, key=lambda x: -bin(x).count("1"))

    x_order = []
    for j in range(bits):
        for order in orders:
            for x in sends(order, j):
                if x not in x_order:
                    x_order.append(x)
    x_order.append(0)

    pl.semaphore_wait(
        barrier,
        (group - 1) + (size_y - 1) + has_before.astype(jnp.int32) + has_after.astype(jnp.int32),
    )

    d2d = {}
    for x in x_order:
        owner_sum(theirs, x, 1 - core)
        d2d[x] = pltpu.make_async_remote_copy(
            src_ref=theirs.at[x],
            dst_ref=partner_in.at[x],
            send_sem=d2d_send.at[x],
            recv_sem=d2d_recv.at[x],
            device_id=partner,
            device_id_type=MESH,
        )
        d2d[x].start()

    group_copies = []
    for k in range(1, group):
        copy = pltpu.make_async_remote_copy(
            src_ref=mass_group.at[0],
            dst_ref=mass_group.at[k],
            send_sem=group_send.at[k],
            recv_sem=group_recv.at[k],
            device_id=at_rank(lax.rem(rank + k, group)),
            device_id_type=MESH,
        )
        copy.start()
        group_copies.append(copy)

    for x in x_order:
        owner_sum(mine, x, core)

    ready = set()

    def prepare(x):
        if x not in ready:
            d2d[x].wait_recv()
            mine[x] = mine[x] + partner_in[x]
            ready.add(x)

    chip_copies = {}

    def take(c, x, j):
        total = mine[x, c]
        for b in orders[c][:j]:
            y = x | (1 << b)
            chip_copies[c, y].wait_recv()
            total = total + chip_in[c, y]
        return total

    leads = (core == 0) == (2 * iy < size_y)

    for j in range(bits):
        if j == 0:

            @pl.when(jnp.logical_not(leads))
            def _():
                pl.semaphore_wait(turn, 1)

        plan = [sends(order, j) for order in orders]
        for i in range(len(plan[0])):
            for c in range(2):
                x = plan[c][i]
                prepare(x)
                if j:
                    mine[x, c] = take(c, x, j)
                copy = pltpu.make_async_remote_copy(
                    src_ref=mine.at[x, c],
                    dst_ref=chip_in.at[c, x],
                    send_sem=chip_send.at[c, x],
                    recv_sem=chip_recv.at[c, x],
                    device_id=at_rank(chip_at(1 << orders[c][j]) * 2 + core),
                    device_id_type=MESH,
                )
                copy.start()
                chip_copies[c, x] = copy
        if j == 0:
            first_sends = list(chip_copies)
            for key in first_sends:
                chip_copies[key].wait_send()

            @pl.when(leads)
            def _():
                pl.semaphore_signal(turn, inc=1, device_id=partner, device_id_type=MESH)

    prepare(0)

    for copy in group_copies:
        copy.wait_recv()
    total = jnp.zeros(mass_group.shape[1:], jnp.float32)
    for a in range(group):
        total = total + mass_group[lax.rem(rank - a + group, group)]
    mass_line[0] = total
    line_copies = []
    for k in range(1, size_y):
        copy = pltpu.make_async_remote_copy(
            src_ref=mass_line.at[0],
            dst_ref=mass_line.at[k],
            send_sem=line_send.at[k],
            recv_sem=line_recv.at[k],
            device_id=(ix, lax.rem(iy + k, size_y), iz),
            device_id_type=MESH,
        )
        copy.start()
        line_copies.append(copy)

    for c in range(2):
        total = take(c, 0, bits)
        for s in range(n_new):
            for f in range(fields):
                new_out[s, f, c * half : (c + 1) * half, :] = total[s, f]

    used = 6 * fields
    tall = faces.shape[1]
    f_row = iota((tall, 2 * rows), 0)
    f_col = iota((tall, 2 * rows), 1)
    f_col = jnp.where(f_col >= rows, f_col - rows, f_col)
    picks = (lax.div(f_row, 6) == lax.div(f_col, edge)) & (f_row < used)
    f_x = lax.rem(f_col, edge)
    gather = jnp.where(picks, 1.0, 0.0).astype(jnp.bfloat16)
    ends = [
        jnp.where(picks & (f_x == at), 1.0, 0.0).astype(jnp.bfloat16) for at in (0, edge - 1)
    ]
    u_row = iota((2 * rows, face), 0)
    u_col = iota((2 * rows, face), 1)
    diagonal = lax.rem(u_row, edge) == lax.div(u_col, edge)
    diagonal = jnp.concatenate([diagonal] * 4, axis=1)
    which = lax.rem(iota((tall, face), 0), 6)
    def face_copy(way, s):
        at = s if way else 2 * n_new + s
        return pltpu.make_async_remote_copy(
            src_ref=ghosts.at[n_new + s],
            dst_ref=ghosts.at[at],
            send_sem=face_send.at[way, s],
            recv_sem=face_recv.at[way, s],
            device_id=at_linear(linear + 1 if way else linear - 1),
            device_id_type=MESH,
        )

    for s in range(n_new):
        high, low = split_two(new_out[s].reshape(rows, face))
        both = jnp.concatenate([high, low], axis=0)
        wide = dot(both, spread[...])
        wide = jnp.where(diagonal, wide, 0.0).astype(jnp.bfloat16)
        sides = dot(gather, wide)
        layers = [dot(ends[0], both), dot(ends[1], both)]
        layers += [sides[:, i * face : (i + 1) * face] for i in range(4)]
        own = layers[0]
        swapped = layers[1]
        for e in range(1, 6):
            own = jnp.where(which == e, layers[e], own)
            swapped = jnp.where(which == e, layers[e ^ 1], swapped)
        faces[s] = own
        ghosts[n_new + s] = swapped

        @pl.when(has_after)
        def _(s=s):
            face_copy(1, s).start()

        @pl.when(has_before)
        def _(s=s):
            face_copy(0, s).start()

    for copy in line_copies:
        copy.wait_recv()
    total = jnp.zeros(mass_group.shape[1:], jnp.float32)
    for a in range(size_y):
        total = total + mass_line[lax.rem(iy - a + size_y, size_y)]
    total = jnp.sum(total, axis=1, keepdims=True) / float(n_old * devices * edge * face)
    m_row = iota((16, 128), 0)
    m_col = iota((16, 128), 1)
    spread_mass = jnp.broadcast_to(total, (16, 128))
    for a in range(2):
        line = jnp.sum(
            jnp.where(m_row == m_col + 8 * a, spread_mass, 0.0)[8 * a : 8 * a + 8],
            axis=0,
            keepdims=True,
        )
        mass_out[a : a + 1, :] = line[:, :fields]

    for x in x_order:
        d2d[x].wait_send()
    for copy in [chip_copies[k] for k in chip_copies if k not in first_sends]:
        copy.wait_send()
    for copy in group_copies + line_copies:
        copy.wait_send()

    @pl.when(has_before)
    def _():
        for s in range(n_new):
            face_copy(1, s).wait_recv()
            face_copy(0, s).wait_send()

    @pl.when(has_after)
    def _():
        for s in range(n_new):
            face_copy(0, s).wait_recv()
            face_copy(1, s).wait_send()

    for s in range(n_new):
        ghost = jnp.zeros((tall, face), jnp.float32)
        present = jnp.zeros((tall, face), jnp.int32)
        for e in range(6):
            side = side_ref[s, e]
            source = linear + side - 1
            here = (side < 3) & (source >= 0) & (source < devices)
            place = jnp.where(side < 3, side, 0) * n_new + patch_ref[s, e]
            ghost = jnp.where(which == e, ghosts[place], ghost)
            present = jnp.where(which == e, here.astype(jnp.int32), present)
        jump = jnp.where(present > 0, ghost - faces[s], 0.0)
        for f in range(fields):
            jump_out[s, f] = jump[6 * f : 6 * f + 6]


def write_out(*refs):
    sems = refs[-1]
    copies = [pltpu.make_async_copy(refs[i], refs[3 + i], sems.at[i]) for i in range(3)]
    for copy in copies:
        copy.start()
    for copy in copies:
        copy.wait()


def body(
    old_data, pair_old, pair_slot, pair_shift, pair_dest, new_ratio, neighbor_side, neighbor_patch
):
    n_old, fields, edge, face = old_data.shape
    n_pairs = pair_old.shape[0]
    n_new = neighbor_side.shape[0]
    size_x, size_y, size_z = (lax.axis_size(a) for a in AXES)
    group = size_x * size_z
    chips = group // 2
    assert size_z % 2 == 0 and chips & (chips - 1) == 0
    half = edge // 2
    tall = -(-6 * fields // 8) * 8
    dims = (size_x, size_y, size_z, n_old, n_new, n_pairs, fields, edge)
    f32 = jnp.float32
    vmem = pl.BlockSpec(memory_space=pltpu.VMEM)
    tables = (pair_old, pair_slot, pair_shift.T, pair_dest.reshape(n_pairs))
    tables += (new_ratio, neighbor_side, neighbor_patch)
    dma = pltpu.SemaphoreType.DMA
    shapes = ((n_new, fields, edge, face), (n_new, fields, 6, face), (2, fields))
    results = pl.pallas_call(
        functools.partial(kernel, dims),
        out_shape=tuple(pltpu.VMEM(s, f32) for s in shapes),
        in_specs=[pl.BlockSpec(memory_space=pl.ANY)] * 8,
        out_specs=(vmem, vmem, vmem),
        scratch_shapes=[pltpu.SMEM(t.shape, jnp.int32) for t in tables]
        + [
            pltpu.VMEM((n_old, fields, edge, face), f32),
            pltpu.VMEM((n_pairs + 1, 2, fields, half, face), f32),
            pltpu.VMEM((chips, 2, n_new, fields, half, face), f32),
            pltpu.VMEM((chips, 2, n_new, fields, half, face), f32),
            pltpu.VMEM((chips, 2, n_new, fields, half, face), f32),
            pltpu.VMEM((2, chips, n_new, fields, half, face), f32),
            pltpu.VMEM((face, 4 * face), jnp.bfloat16),
            pltpu.VMEM((n_new, tall, face), f32),
            pltpu.VMEM((3 * n_new, tall, face), f32),
            pltpu.VMEM((group, 16, 128), f32),
            pltpu.VMEM((size_y, 16, 128), f32),
            dma,
            dma((len(tables),)),
            pltpu.SemaphoreType.REGULAR,
            dma((chips,)),
            dma((chips,)),
            dma((2, chips)),
            dma((2, chips)),
            dma((2, n_new)),
            dma((2, n_new)),
            dma((group,)),
            dma((group,)),
            dma((size_y,)),
            dma((size_y,)),
        ],
        compiler_params=pltpu.CompilerParams(collective_id=0, has_side_effects=True),
    )(old_data, *tables)
    return pl.pallas_call(
        write_out,
        out_shape=tuple(jax.ShapeDtypeStruct(s, f32) for s in shapes),
        in_specs=[vmem] * 3,
        out_specs=(pl.BlockSpec(memory_space=pl.ANY),) * 3,
        scratch_shapes=[dma((3,))],
    )(*(pltpu.with_memory_space_constraint(r, pltpu.VMEM) for r in results))


def solution(mesh):
    whole = P(AXES)
    return jax.shard_map(
        body,
        mesh=mesh,
        in_specs=(whole, whole, whole, whole, whole, P(), whole, whole),
        out_specs=(whole, whole, P()),
        check_vma=False,
    )
```

profile of v0, /device:TPU:0, one launch (start us, length us, event | category | flops | bytes accessed | tf_op | source)
XLA Modules:
  0.0 23.6 jit_solution(3188044834219845635)
XLA Ops:
  0.6 22.2 %shard_map.103 = (f32[3,5,16,256]{3,2,1,0:T(8,128)S(1)}, f32[3,5,6,256]{3,2,1,0:T(8,128)S(1)}, f32[2,5]{1,0:T(2,128)S(1)}) custom-call(f32[12,5,16,256]{3,2,1,0:T(8,128)} %old_hbm.1, s32[8]{0:T(128)} %pair_old_hbm.1, s32[8]{0:T(128)} %pair_slot_hbm.1, s32[3,8]{1,0:T(4,128)} %bitcast.2, s32[8]{0:T(128)} %bitcast.3, s32[96]{0:T(128)} %new_ratio_hbm.1, ...), custom_call_target="tpu_custom_call" | custom-call | tf_op jit(solution)/shard_map/pallas_call | solution.py:496
  22.8 0.8 %shard_map.104 = (f32[3,5,16,256]{3,2,1,0:T(8,128)}, f32[3,5,6,256]{3,2,1,0:T(8,128)}, f32[2,5]{1,0:T(2,128)}) custom-call(f32[3,5,16,256]{3,2,1,0:T(8,128)S(1)} %get-tuple-element.6.refs_0_, f32[3,5,6,256]{3,2,1,0:T(8,128)S(1)} %get-tuple-element.7.refs_1_, f32[2,5]{1,0:T(2,128)S(1)} %get-tuple-element.8.refs_2_), custom_call_target="tpu_custom_call" | custom-call | tf_op jit(solution)/shard_map/pallas_call | solution.py:530
where the time goes:
time: 23.7 us; the launch traced here: 23.6 us
  Pallas kernels  22.9 us (97%)
  between operations  0.64 us (3%)
    pallas_call x1, Pallas kernels, body(): pl.pallas_call(functools.partial(kernel, dims), out_shape=tuple((pltpu.VM...  22.2 us
    pallas_call x1, Pallas kernels, body(): pl.pallas_call(write_out, out_shape=tuple((jax.ShapeDtypeStruct(s, f32) f...  0.76 us

commit v1 on v0

--- a/solution.py
+++ b/solution.py
@@ -9,6 +9,7 @@
 
 MESH = pl.DeviceIdType.MESH
 AXES = ("gx", "gy", "gz")
+TURN_STEP = 9
 
 
 def split_two(value):
@@ -23,6 +24,25 @@
 
 def iota(shape, axis):
     return lax.broadcasted_iota(jnp.int32, shape, axis)
+
+
+def plan_of(bits, n_new):
+    chips = 1 << bits
+    orders = [list(range(bits)), list(reversed(range(bits)))]
+
+    def sends(order, j):
+        done = sum(1 << b for b in order[:j])
+        xs = [x for x in range(chips) if (x >> order[j]) & 1 and not x & done]
+        return sorted(xs, key=lambda x: -bin(x).count("1"))
+
+    steps = []
+    for j in range(bits):
+        for pair in zip(*(sends(order, j) for order in orders)):
+            fine = j == bits - 1 or pair[0] == chips - 1
+            for s in range(n_new) if fine else [None]:
+                for c in range(2):
+                    steps.append((j, c, pair[c], s))
+    return orders, steps
 
 
 def kernel(
@@ -59,6 +79,8 @@
     old_sem,
     table_sem,
     turn,
+    row_ready,
+    far_ready,
     d2d_send,
     d2d_recv,
     chip_send,
@@ -104,6 +126,13 @@
     has_before = linear > 0
     has_after = linear < devices - 1
     partner = at_rank(chip * 2 + 1 - core)
+    last_z = iz == size_z - 1
+    first_z = iz == 0
+    last_y = iy == size_y - 1
+    first_y = iy == 0
+
+    def signal(sem, device):
+        pl.semaphore_signal(sem, inc=1, device_id=device, device_id_type=MESH)
 
     old_copy = pltpu.make_async_copy(old_hbm, old, old_sem)
     old_copy.start()
@@ -124,22 +153,47 @@
         table.start()
 
     barrier = pltpu.get_barrier_semaphore()
-    for k in range(1, group):
-        pl.semaphore_signal(
-            barrier, inc=1, device_id=at_rank(lax.rem(rank + k, group)), device_id_type=MESH
-        )
-    for k in range(1, size_y):
-        pl.semaphore_signal(
-            barrier, inc=1, device_id=(ix, lax.rem(iy + k, size_y), iz), device_id_type=MESH
-        )
-
-    @pl.when(has_before)
-    def _():
-        pl.semaphore_signal(barrier, inc=1, device_id=at_linear(linear - 1), device_id_type=MESH)
-
-    @pl.when(has_after)
-    def _():
-        pl.semaphore_signal(barrier, inc=1, device_id=at_linear(linear + 1), device_id_type=MESH)
+    signal(barrier, partner)
+
+    @pl.loop(2 * chip + 2, group)
+    def _(r):
+        signal(barrier, at_rank(r))
+
+    @pl.loop(iy + 1, size_y)
+    def _(y):
+        signal(barrier, (ix, y, iz))
+
+    up = last_z & (iy < size_y - 1)
+    down = first_z & (iy > 0)
+    turn_after = last_z & last_y & has_after
+    turn_before = first_z & first_y & has_before
+
+    @pl.when(up)
+    def _():
+        signal(barrier, at_linear(linear + 1))
+
+    @pl.when(turn_before)
+    def _():
+        signal(barrier, at_linear(linear - 1))
+
+    count = 1 + 2 * chip + iy + down.astype(jnp.int32) + turn_after.astype(jnp.int32)
+    pl.semaphore_wait(barrier, count)
+
+    @pl.loop(0, 2 * chip)
+    def _(r):
+        signal(row_ready, at_rank(r))
+
+    @pl.loop(0, iy)
+    def _(y):
+        signal(far_ready, (ix, y, iz))
+
+    @pl.when(down)
+    def _():
+        signal(far_ready, at_linear(linear - 1))
+
+    @pl.when(turn_after)
+    def _():
+        signal(far_ready, at_linear(linear + 1))
 
     col = iota((face, face), 1)
     row = iota((face, face), 0)
@@ -211,157 +265,177 @@
                 parts[p, c, f] = piece
                 new_acc[f] = new_acc[f] + cube * piece
 
+    def owner_sum(dst, x, s, core_of):
+        target = chip_at(x) * 2 + core_of
+        wanted = target * n_new + s
+        first = jnp.int32(n_pairs)
+        second = jnp.int32(n_pairs)
+        for p in reversed(range(n_pairs)):
+            hit = keys[p] == wanted
+            second = jnp.where(hit, first, second)
+            first = jnp.where(hit, jnp.int32(p), first)
+        dst[x, :, s] = parts[first] + parts[second]
+
+    orders, steps = plan_of(bits, n_new)
+
+    def d2d_key(x, s):
+        return (x, s) if x == chips - 1 else (x, None)
+
+    d2d_order = []
+    for _, _, x, s in steps:
+        for t in range(n_new) if s is None else [s]:
+            if d2d_key(x, t) not in d2d_order:
+                d2d_order.append(d2d_key(x, t))
+    d2d_order.append((0, None))
+
+    def to_partner(key):
+        x, s = key
+        at = (x, slice(None), s) if s is not None else (x,)
+        return pltpu.make_async_remote_copy(
+            src_ref=theirs.at[at],
+            dst_ref=partner_in.at[at],
+            send_sem=d2d_send,
+            recv_sem=d2d_recv.at[d2d_order.index(key)],
+            device_id=partner,
+            device_id_type=MESH,
+        )
+
+    for x, s in d2d_order:
+        for t in range(n_new) if s is None else [s]:
+            owner_sum(theirs, x, t, 1 - core)
+        to_partner((x, s)).start()
+
+    for x, s in d2d_order:
+        for t in range(n_new) if s is None else [s]:
+            owner_sum(mine, x, t, core)
+
+    m_row = iota((16, 128), 0)
+    m_col = iota((16, 128), 1)
     zero_rows = jnp.zeros((8 - fields, 128), jnp.float32)
 
     def lines(accs):
         out = [
             jnp.sum(a[:, :128] + a[:, 128:], axis=0, keepdims=True) for a in accs
         ]
-        return jnp.concatenate(out + [zero_rows], axis=0)
-
-    mass_group[0, 0:8] = lines(old_acc)
-    mass_group[0, 8:16] = lines(new_acc)
-
-    def owner_sum(dst, x, core_of):
-        target = chip_at(x) * 2 + core_of
-        for s in range(n_new):
-            wanted = target * n_new + s
-            first = jnp.int32(n_pairs)
-            second = jnp.int32(n_pairs)
-            for p in reversed(range(n_pairs)):
-                hit = keys[p] == wanted
-                second = jnp.where(hit, first, second)
-                first = jnp.where(hit, jnp.int32(p), first)
-            dst[x, :, s] = parts[first] + parts[second]
-
-    orders = [list(range(bits)), list(reversed(range(bits)))]
-
-    def sends(order, j):
-        done = sum(1 << b for b in order[:j])
-        xs = [x for x in range(chips) if (x >> order[j]) & 1 and not x & done]
-        return sorted(xs, key=lambda x: -bin(x).count("1"))
-
-    x_order = []
-    for j in range(bits):
-        for order in orders:
-            for x in sends(order, j):
-                if x not in x_order:
-                    x_order.append(x)
-    x_order.append(0)
-
-    pl.semaphore_wait(
-        barrier,
-        (group - 1) + (size_y - 1) + has_before.astype(jnp.int32) + has_after.astype(jnp.int32),
-    )
-
-    d2d = {}
-    for x in x_order:
-        owner_sum(theirs, x, 1 - core)
-        d2d[x] = pltpu.make_async_remote_copy(
-            src_ref=theirs.at[x],
-            dst_ref=partner_in.at[x],
-            send_sem=d2d_send.at[x],
-            recv_sem=d2d_recv.at[x],
+        return out + [zero_rows]
+
+    sums = jnp.concatenate(lines(old_acc) + lines(new_acc), axis=0)
+    sums = jnp.sum(sums, axis=1, keepdims=True)
+    sums = jnp.where(m_row == m_col, jnp.broadcast_to(sums, (16, 128)), 0.0)
+    mass_group[0] = jnp.sum(sums, axis=0, keepdims=True)
+
+    landed, joined = set(), set()
+
+    def prepare(x, s):
+        key = d2d_key(x, s)
+        if key not in landed:
+            landed.add(key)
+            to_partner(key).wait_recv()
+        if (x, s) not in joined:
+            joined.add((x, s))
+            mine[x, :, s] = mine[x, :, s] + partner_in[x, :, s]
+
+    def to_chip(step):
+        j, c, x, s = step
+        here = (x, c) if s is None else (x, c, s)
+        there = (x - 1, c) if s is None else (x - 1, c, s)
+        return pltpu.make_async_remote_copy(
+            src_ref=mine.at[here],
+            dst_ref=chip_in.at[there],
+            send_sem=chip_send,
+            recv_sem=chip_recv.at[steps.index(step)],
+            device_id=at_rank(chip_at(1 << orders[c][j]) * 2 + core),
+            device_id_type=MESH,
+        )
+
+    waited = set()
+
+    def take(c, x, s, j):
+        total = mine[x, c, s]
+        for b in orders[c][:j]:
+            y = x | (1 << b)
+            step = next(t for t in steps if t[1:3] == (c, y) and t[3] in (None, s))
+            if step not in waited:
+                waited.add(step)
+                to_chip(step).wait_recv()
+            total = total + chip_in[y - 1, c, s]
+        return total
+
+    leads = (core == 0) == (2 * iy < size_y)
+    prepare(steps[0][2], 0)
+
+    above = group - 2 * (chip + 1)
+
+    @pl.when(above > 0)
+    def _():
+        pl.semaphore_wait(row_ready, above)
+
+    def to_group(k):
+        return pltpu.make_async_remote_copy(
+            src_ref=mass_group.at[0],
+            dst_ref=mass_group.at[k],
+            send_sem=group_send,
+            recv_sem=group_recv,
+            device_id=at_rank(lax.rem(rank + k, group)),
+            device_id_type=MESH,
+        )
+
+    for k in range(1, group):
+        to_group(k).start()
+
+    @pl.when(jnp.logical_not(leads))
+    def _():
+        pl.semaphore_wait(turn, 1)
+
+    for n, step in enumerate(steps):
+        j, c, x, s = step
+        for t in range(n_new) if s is None else [s]:
+            prepare(x, t)
+            if j:
+                mine[x, c, t] = take(c, x, t, j)
+        to_chip(step).start()
+        if n == TURN_STEP:
+
+            @pl.when(leads)
+            def _():
+                signal(turn, partner)
+
+    for s in range(n_new):
+        prepare(0, s)
+
+    def all_of(ref, send_sem, recv_sem):
+        return pltpu.make_async_remote_copy(
+            src_ref=ref,
+            dst_ref=ref,
+            send_sem=send_sem,
+            recv_sem=recv_sem,
             device_id=partner,
             device_id_type=MESH,
         )
-        d2d[x].start()
-
-    group_copies = []
-    for k in range(1, group):
-        copy = pltpu.make_async_remote_copy(
-            src_ref=mass_group.at[0],
-            dst_ref=mass_group.at[k],
-            send_sem=group_send.at[k],
-            recv_sem=group_recv.at[k],
-            device_id=at_rank(lax.rem(rank + k, group)),
-            device_id_type=MESH,
-        )
-        copy.start()
-        group_copies.append(copy)
-
-    for x in x_order:
-        owner_sum(mine, x, core)
-
-    ready = set()
-
-    def prepare(x):
-        if x not in ready:
-            d2d[x].wait_recv()
-            mine[x] = mine[x] + partner_in[x]
-            ready.add(x)
-
-    chip_copies = {}
-
-    def take(c, x, j):
-        total = mine[x, c]
-        for b in orders[c][:j]:
-            y = x | (1 << b)
-            chip_copies[c, y].wait_recv()
-            total = total + chip_in[c, y]
-        return total
-
-    leads = (core == 0) == (2 * iy < size_y)
-
-    for j in range(bits):
-        if j == 0:
-
-            @pl.when(jnp.logical_not(leads))
-            def _():
-                pl.semaphore_wait(turn, 1)
-
-        plan = [sends(order, j) for order in orders]
-        for i in range(len(plan[0])):
-            for c in range(2):
-                x = plan[c][i]
-                prepare(x)
-                if j:
-                    mine[x, c] = take(c, x, j)
-                copy = pltpu.make_async_remote_copy(
-                    src_ref=mine.at[x, c],
-                    dst_ref=chip_in.at[c, x],
-                    send_sem=chip_send.at[c, x],
-                    recv_sem=chip_recv.at[c, x],
-                    device_id=at_rank(chip_at(1 << orders[c][j]) * 2 + core),
-                    device_id_type=MESH,
-                )
-                copy.start()
-                chip_copies[c, x] = copy
-        if j == 0:
-            first_sends = list(chip_copies)
-            for key in first_sends:
-                chip_copies[key].wait_send()
-
-            @pl.when(leads)
-            def _():
-                pl.semaphore_signal(turn, inc=1, device_id=partner, device_id_type=MESH)
-
-    prepare(0)
-
-    for copy in group_copies:
-        copy.wait_recv()
+
+    every_group = all_of(mass_group.at[1:], group_send, group_recv)
+    every_group.wait_recv()
     total = jnp.zeros(mass_group.shape[1:], jnp.float32)
     for a in range(group):
         total = total + mass_group[lax.rem(rank - a + group, group)]
     mass_line[0] = total
-    line_copies = []
+
+    beyond = size_y - 1 - iy + up.astype(jnp.int32) + turn_before.astype(jnp.int32)
+
+    @pl.when(beyond > 0)
+    def _():
+        pl.semaphore_wait(far_ready, beyond)
+
     for k in range(1, size_y):
-        copy = pltpu.make_async_remote_copy(
+        pltpu.make_async_remote_copy(
             src_ref=mass_line.at[0],
             dst_ref=mass_line.at[k],
-            send_sem=line_send.at[k],
-            recv_sem=line_recv.at[k],
+            send_sem=line_send,
+            recv_sem=line_recv,
             device_id=(ix, lax.rem(iy + k, size_y), iz),
             device_id_type=MESH,
-        )
-        copy.start()
-        line_copies.append(copy)
-
-    for c in range(2):
-        total = take(c, 0, bits)
-        for s in range(n_new):
-            for f in range(fields):
-                new_out[s, f, c * half : (c + 1) * half, :] = total[s, f]
+        ).start()
+    every_line = all_of(mass_line.at[1:], line_send, line_recv)
 
     used = 6 * fields
     tall = faces.shape[1]
@@ -379,18 +453,26 @@
     diagonal = lax.rem(u_row, edge) == lax.div(u_col, edge)
     diagonal = jnp.concatenate([diagonal] * 4, axis=1)
     which = lax.rem(iota((tall, face), 0), 6)
+
     def face_copy(way, s):
-        at = s if way else 2 * n_new + s
+        from_at, to_at = pl.ds(n_new, n_new), pl.ds(0 if way else 2 * n_new, n_new)
+        if s is not None:
+            from_at, to_at = n_new + s, s if way else 2 * n_new + s
         return pltpu.make_async_remote_copy(
-            src_ref=ghosts.at[n_new + s],
-            dst_ref=ghosts.at[at],
-            send_sem=face_send.at[way, s],
-            recv_sem=face_recv.at[way, s],
+            src_ref=ghosts.at[from_at],
+            dst_ref=ghosts.at[to_at],
+            send_sem=face_send.at[way],
+            recv_sem=face_recv.at[way],
             device_id=at_linear(linear + 1 if way else linear - 1),
             device_id_type=MESH,
         )
 
+
     for s in range(n_new):
+        for c in range(2):
+            total = take(c, 0, s, bits)
+            for f in range(fields):
+                new_out[s, f, c * half : (c + 1) * half, :] = total[f]
         high, low = split_two(new_out[s].reshape(rows, face))
         both = jnp.concatenate([high, low], axis=0)
         wide = dot(both, spread[...])
@@ -414,41 +496,28 @@
         def _(s=s):
             face_copy(0, s).start()
 
-    for copy in line_copies:
-        copy.wait_recv()
+    every_line.wait_recv()
     total = jnp.zeros(mass_group.shape[1:], jnp.float32)
     for a in range(size_y):
         total = total + mass_line[lax.rem(iy - a + size_y, size_y)]
-    total = jnp.sum(total, axis=1, keepdims=True) / float(n_old * devices * edge * face)
-    m_row = iota((16, 128), 0)
-    m_col = iota((16, 128), 1)
-    spread_mass = jnp.broadcast_to(total, (16, 128))
+    total = total / float(n_old * devices * edge * face)
     for a in range(2):
-        line = jnp.sum(
-            jnp.where(m_row == m_col + 8 * a, spread_mass, 0.0)[8 * a : 8 * a + 8],
-            axis=0,
-            keepdims=True,
-        )
-        mass_out[a : a + 1, :] = line[:, :fields]
-
-    for x in x_order:
-        d2d[x].wait_send()
-    for copy in [chip_copies[k] for k in chip_copies if k not in first_sends]:
-        copy.wait_send()
-    for copy in group_copies + line_copies:
-        copy.wait_send()
+        mass_out[a : a + 1, :] = total[:, 8 * a : 8 * a + fields]
+
+    all_of(theirs, d2d_send, d2d_recv.at[0]).wait_send()
+    all_of(chip_in, chip_send, chip_recv.at[0]).wait_send()
+    every_group.wait_send()
+    every_line.wait_send()
 
     @pl.when(has_before)
     def _():
-        for s in range(n_new):
-            face_copy(1, s).wait_recv()
-            face_copy(0, s).wait_send()
+        face_copy(1, None).wait_recv()
+        face_copy(0, None).wait_send()
 
     @pl.when(has_after)
     def _():
-        for s in range(n_new):
-            face_copy(0, s).wait_recv()
-            face_copy(1, s).wait_send()
+        face_copy(0, None).wait_recv()
+        face_copy(1, None).wait_send()
 
     for s in range(n_new):
         ghost = jnp.zeros((tall, face), jnp.float32)
@@ -485,6 +554,7 @@
     chips = group // 2
     assert size_z % 2 == 0 and chips & (chips - 1) == 0
     half = edge // 2
+    bits = chips.bit_length() - 1
     tall = -(-6 * fields // 8) * 8
     dims = (size_x, size_y, size_z, n_old, n_new, n_pairs, fields, edge)
     f32 = jnp.float32
@@ -505,25 +575,27 @@
             pltpu.VMEM((chips, 2, n_new, fields, half, face), f32),
             pltpu.VMEM((chips, 2, n_new, fields, half, face), f32),
             pltpu.VMEM((chips, 2, n_new, fields, half, face), f32),
-            pltpu.VMEM((2, chips, n_new, fields, half, face), f32),
+            pltpu.VMEM((chips - 1, 2, n_new, fields, half, face), f32),
             pltpu.VMEM((face, 4 * face), jnp.bfloat16),
             pltpu.VMEM((n_new, tall, face), f32),
             pltpu.VMEM((3 * n_new, tall, face), f32),
-            pltpu.VMEM((group, 16, 128), f32),
-            pltpu.VMEM((size_y, 16, 128), f32),
+            pltpu.VMEM((group, 1, 128), f32),
+            pltpu.VMEM((size_y, 1, 128), f32),
             dma,
             dma((len(tables),)),
             pltpu.SemaphoreType.REGULAR,
-            dma((chips,)),
-            dma((chips,)),
-            dma((2, chips)),
-            dma((2, chips)),
-            dma((2, n_new)),
-            dma((2, n_new)),
-            dma((group,)),
-            dma((group,)),
-            dma((size_y,)),
-            dma((size_y,)),
+            pltpu.SemaphoreType.REGULAR,
+            pltpu.SemaphoreType.REGULAR,
+            dma,
+            dma((n_new + chips - 1,)),
+            dma,
+            dma((len(plan_of(bits, n_new)[1]),)),
+            dma((2,)),
+            dma((2,)),
+            dma,
+            dma,
+            dma,
+            dma,
         ],
         compiler_params=pltpu.CompilerParams(collective_id=0, has_side_effects=True),
     )(old_data, *tables)

time: 23.7 us -> 20.9 us (0.88)
  the two profiles are of different devices: /device:TPU:0 before, /device:TPU:19 now
where the time goes in v1:
time: 20.9 us; the launch traced here: 20.7 us
  Pallas kernels  20.1 us (96%)
  between operations  0.64 us (3%)
    pallas_call x1, Pallas kernels, body(): pl.pallas_call(functools.partial(kernel, dims), out_shape=tuple((pltpu.VM...  19.3 us
    pallas_call x1, Pallas kernels, body(): pl.pallas_call(write_out, out_shape=tuple((jax.ShapeDtypeStruct(s, f32) f...  0.76 us

profile of v1, /device:TPU:19, one launch (start us, length us, event | category | flops | bytes accessed | tf_op | source)
XLA Modules:
  0.0 20.7 jit_solution(16519743644212779347)
XLA Ops:
  0.6 19.3 %shard_map.103 = (f32[3,5,16,256]{3,2,1,0:T(8,128)S(1)}, f32[3,5,6,256]{3,2,1,0:T(8,128)S(1)}, f32[2,5]{1,0:T(2,128)S(1)}) custom-call(f32[12,5,16,256]{3,2,1,0:T(8,128)} %old_hbm.1, s32[8]{0:T(128)} %pair_old_hbm.1, s32[8]{0:T(128)} %pair_slot_hbm.1, s32[3,8]{1,0:T(4,128)} %bitcast.2, s32[8]{0:T(128)} %bitcast.3, s32[96]{0:T(128)} %new_ratio_hbm.1, ...), custom_call_target="tpu_custom_call" | custom-call | tf_op jit(solution)/shard_map/pallas_call | solution.py:566
  19.9 0.8 %shard_map.104 = (f32[3,5,16,256]{3,2,1,0:T(8,128)}, f32[3,5,6,256]{3,2,1,0:T(8,128)}, f32[2,5]{1,0:T(2,128)}) custom-call(f32[3,5,16,256]{3,2,1,0:T(8,128)S(1)} %get-tuple-element.6.refs_0_, f32[3,5,6,256]{3,2,1,0:T(8,128)S(1)} %get-tuple-element.7.refs_1_, f32[2,5]{1,0:T(2,128)S(1)} %get-tuple-element.8.refs_2_), custom_call_target="tpu_custom_call" | custom-call | tf_op jit(solution)/shard_map/pallas_call | solution.py:602

commit v2 on v1

--- a/solution.py
+++ b/solution.py
@@ -9,7 +9,10 @@
 
 MESH = pl.DeviceIdType.MESH
 AXES = ("gx", "gy", "gz")
-TURN_STEP = 9
+TURN_AT = 2
+TURN_LAST = 1
+EARLY_X1 = True
+LEAD_MODE = 1
 
 
 def split_two(value):
@@ -65,21 +68,23 @@
     new_ratio,
     side_ref,
     patch_ref,
+    gap,
+    near_x,
     old,
     parts,
     mine,
     theirs,
     partner_in,
     chip_in,
-    spread,
     faces,
     ghosts,
-    mass_group,
+    mass_own,
+    mass_in,
     mass_line,
     old_sem,
     table_sem,
     turn,
-    row_ready,
+    near,
     far_ready,
     d2d_send,
     d2d_recv,
@@ -87,8 +92,8 @@
     chip_recv,
     face_send,
     face_recv,
-    group_send,
-    group_recv,
+    mass_send,
+    mass_recv,
     line_send,
     line_recv,
 ):
@@ -152,22 +157,31 @@
     for table in tables:
         table.start()
 
+    def bit(b):
+        return lax.rem(lax.div(chip, 1 << b), 2)
+
+    def near_chip(b):
+        return at_rank(chip_at(1 << b) * 2 + core)
+
+    end = last_z & last_y
+    start = first_z & first_y
+    up = (core == 1) & has_after & jnp.logical_not(end)
+    down = (core == 0) & has_before & jnp.logical_not(start)
+    turn_after = end & has_after
+    turn_before = start & has_before
+
     barrier = pltpu.get_barrier_semaphore()
     signal(barrier, partner)
-
-    @pl.loop(2 * chip + 2, group)
-    def _(r):
-        signal(barrier, at_rank(r))
+    for b in range(bits):
+
+        @pl.when(bit(b) == 0)
+        def _(b=b):
+            signal(barrier, near_chip(b))
 
     @pl.loop(iy + 1, size_y)
     def _(y):
         signal(barrier, (ix, y, iz))
 
-    up = last_z & (iy < size_y - 1)
-    down = first_z & (iy > 0)
-    turn_after = last_z & last_y & has_after
-    turn_before = first_z & first_y & has_before
-
     @pl.when(up)
     def _():
         signal(barrier, at_linear(linear + 1))
@@ -176,34 +190,37 @@
     def _():
         signal(barrier, at_linear(linear - 1))
 
-    count = 1 + 2 * chip + iy + down.astype(jnp.int32) + turn_after.astype(jnp.int32)
-    pl.semaphore_wait(barrier, count)
-
-    @pl.loop(0, 2 * chip)
-    def _(r):
-        signal(row_ready, at_rank(r))
-
-    @pl.loop(0, iy)
-    def _(y):
-        signal(far_ready, (ix, y, iz))
-
-    @pl.when(down)
-    def _():
-        signal(far_ready, at_linear(linear - 1))
-
-    @pl.when(turn_after)
-    def _():
-        signal(far_ready, at_linear(linear + 1))
+    count = 1 + iy + down.astype(jnp.int32) + turn_after.astype(jnp.int32)
+    for b in range(bits):
+        count = count + bit(b)
+
+    def greet():
+        pl.semaphore_wait(barrier, count)
+        for b in range(bits):
+
+            @pl.when(bit(b) == 1)
+            def _(b=b):
+                signal(near.at[b], near_chip(b))
+
+        @pl.loop(0, iy)
+        def _(y):
+            signal(far_ready, (ix, y, iz))
+
+        @pl.when(down)
+        def _():
+            signal(far_ready, at_linear(linear - 1))
+
+        @pl.when(turn_after)
+        def _():
+            signal(far_ready, at_linear(linear + 1))
+
+    pl.when(jnp.logical_not(turn_after))(greet)
 
     col = iota((face, face), 1)
     row = iota((face, face), 0)
-    low_col = lax.rem(col, edge)
-    for i, wanted in enumerate(
-        (low_col, low_col + face - edge, low_col * edge, low_col * edge + edge - 1)
-    ):
-        spread[:, i * face : (i + 1) * face] = jnp.where(row == wanted, 1.0, 0.0).astype(
-            jnp.bfloat16
-        )
+    for s in range(n_new):
+        ghosts[n_new + s] = jnp.zeros(ghosts.shape[1:], jnp.float32)
+        faces[s] = jnp.zeros(faces.shape[1:], jnp.float32)
 
     @pl.when(jnp.logical_not(has_before))
     def _():
@@ -212,6 +229,21 @@
     @pl.when(jnp.logical_not(has_after))
     def _():
         ghosts[2 * n_new :] = jnp.zeros((n_new, *ghosts.shape[1:]), jnp.float32)
+
+    wide = 4 * edge
+    l_row = iota((rows, 2 * rows), 0)
+    l_col = iota((rows, 2 * rows), 1)
+    l_col = jnp.where(l_col >= rows, l_col - rows, l_col)
+    same_field = lax.div(l_row, edge) == lax.div(l_col, edge)
+    for r in (1, 2):
+        gap[r - 1] = (
+            (lax.div(row, edge) - r * lax.div(col, edge)) * wide
+            + lax.rem(row, edge)
+            - r * lax.rem(col, edge)
+        )
+        near_x[r - 1] = jnp.where(
+            same_field, lax.rem(l_col, edge) - r * lax.rem(l_row, edge), wide
+        )
 
     for table in tables:
         table.wait()
@@ -223,15 +255,6 @@
         ratios.append(new_ratio[owner * n_new + pair_slot[p]])
 
     parts[n_pairs] = jnp.zeros(parts.shape[1:], jnp.float32)
-    row_y = lax.div(row, edge)
-    row_z = lax.rem(row, edge)
-    l_row = iota((rows, 2 * rows), 0)
-    l_col = iota((rows, 2 * rows), 1)
-    l_col = jnp.where(l_col >= rows, l_col - rows, l_col)
-    same_field = lax.div(l_row, edge) == lax.div(l_col, edge)
-    l_i = lax.rem(l_row, edge)
-    l_m = lax.rem(l_col, edge)
-
     old_copy.wait()
 
     old_acc = [jnp.zeros((8, face), jnp.float32) for _ in range(fields)]
@@ -244,26 +267,28 @@
     for p in range(n_pairs):
         ratio = ratios[p]
         coarse = ratio == 2
-        step = ratio - 1
+        kind = coarse.astype(jnp.int32)
         tx, ty, tz = pair_shift[0, p], pair_shift[1, p], pair_shift[2, p]
         scale = jnp.where(coarse, jnp.float32(0.125), jnp.float32(1.0))
         cube = jnp.where(coarse, jnp.float32(8.0), jnp.float32(1.0))
+        inside = jnp.where(coarse, -2, -1)
+        both_inside = jnp.where(coarse, -2 - wide, -1)
         block = old[pair_old[p]].reshape(rows, face)
-        lx = (lax.shift_right_arithmetic(l_m - tx, jnp.full_like(l_m, step)) == l_i) & same_field
+        lx = ((near_x[kind] - tx) & inside) == 0
         lx = jnp.where(lx, 1.0, 0.0).astype(jnp.bfloat16)
         high, low = split_two(block)
         mixed = dot(lx, jnp.concatenate([high, low], axis=0))
-        ky = lax.shift_right_arithmetic(row_y - ty, jnp.full_like(row, step))
-        kz = lax.shift_right_arithmetic(row_z - tz, jnp.full_like(row, step))
-        code = jnp.where((kz >= 0) & (kz < edge), ky * edge + kz, -1)
-        weight = jnp.where(code == col, scale, jnp.float32(0.0)).astype(jnp.bfloat16)
-        high, low = split_two(mixed)
-        out = dot(high, weight) + dot(low, weight)
+        weight = ((gap[kind] - (ty * wide + tz)) & both_inside) == 0
+        weight = jnp.where(weight, scale, jnp.float32(0.0)).astype(jnp.bfloat16)
+        out = dot(jnp.concatenate(split_two(mixed), axis=0), weight)
+        out = out[:rows] + out[rows:]
         for f in range(fields):
             for c in range(2):
                 piece = out[f * edge + c * half : f * edge + (c + 1) * half]
                 parts[p, c, f] = piece
                 new_acc[f] = new_acc[f] + cube * piece
+
+    pl.when(turn_after)(greet)
 
     def owner_sum(dst, x, s, core_of):
         target = chip_at(x) * 2 + core_of
@@ -300,14 +325,13 @@
             device_id_type=MESH,
         )
 
-    for x, s in d2d_order:
-        for t in range(n_new) if s is None else [s]:
-            owner_sum(theirs, x, t, 1 - core)
-        to_partner((x, s)).start()
-
-    for x, s in d2d_order:
-        for t in range(n_new) if s is None else [s]:
-            owner_sum(mine, x, t, core)
+    def send_theirs(keys):
+        for x, s in keys:
+            for t in range(n_new) if s is None else [s]:
+                owner_sum(theirs, x, t, 1 - core)
+            to_partner((x, s)).start()
+
+    send_theirs(d2d_order[:n_new])
 
     m_row = iota((16, 128), 0)
     m_col = iota((16, 128), 1)
@@ -322,7 +346,29 @@
     sums = jnp.concatenate(lines(old_acc) + lines(new_acc), axis=0)
     sums = jnp.sum(sums, axis=1, keepdims=True)
     sums = jnp.where(m_row == m_col, jnp.broadcast_to(sums, (16, 128)), 0.0)
-    mass_group[0] = jnp.sum(sums, axis=0, keepdims=True)
+    mass_own[0] = jnp.sum(sums, axis=0, keepdims=True)
+
+    def mass_copy(k):
+        return pltpu.make_async_remote_copy(
+            src_ref=mass_own.at[k],
+            dst_ref=mass_in.at[k],
+            send_sem=mass_send.at[k],
+            recv_sem=mass_recv.at[k],
+            device_id=near_chip(k - 1) if k else partner,
+            device_id_type=MESH,
+        )
+
+    def mass_join(k):
+        mass_copy(k).wait_recv()
+        mass_own[k + 1] = mass_own[k] + mass_in[k]
+
+    mass_copy(0).start()
+
+    send_theirs(d2d_order[n_new:])
+
+    for x, s in d2d_order:
+        for t in range(n_new) if s is None else [s]:
+            owner_sum(mine, x, t, core)
 
     landed, joined = set(), set()
 
@@ -362,46 +408,27 @@
         return total
 
     leads = (core == 0) == (2 * iy < size_y)
+    if LEAD_MODE == 1:
+        leads = (core == 0) == (iy < size_y - 1)
+    if LEAD_MODE == 2:
+        leads = core == 0
     prepare(steps[0][2], 0)
 
-    above = group - 2 * (chip + 1)
-
-    @pl.when(above > 0)
-    def _():
-        pl.semaphore_wait(row_ready, above)
-
-    def to_group(k):
-        return pltpu.make_async_remote_copy(
-            src_ref=mass_group.at[0],
-            dst_ref=mass_group.at[k],
-            send_sem=group_send,
-            recv_sem=group_recv,
-            device_id=at_rank(lax.rem(rank + k, group)),
-            device_id_type=MESH,
-        )
-
-    for k in range(1, group):
-        to_group(k).start()
-
-    @pl.when(jnp.logical_not(leads))
-    def _():
-        pl.semaphore_wait(turn, 1)
-
-    for n, step in enumerate(steps):
-        j, c, x, s = step
-        for t in range(n_new) if s is None else [s]:
-            prepare(x, t)
-            if j:
-                mine[x, c, t] = take(c, x, t, j)
-        to_chip(step).start()
-        if n == TURN_STEP:
-
-            @pl.when(leads)
+    met = set()
+
+    def meet(b):
+        if b not in met:
+            met.add(b)
+
+            @pl.when(bit(b) == 0)
             def _():
-                signal(turn, partner)
-
-    for s in range(n_new):
-        prepare(0, s)
+                pl.semaphore_wait(near.at[b], 1)
+
+    meet(0)
+
+    def mass_first():
+        mass_join(0)
+        mass_copy(1).start()
 
     def all_of(ref, send_sem, recv_sem):
         return pltpu.make_async_remote_copy(
@@ -413,46 +440,129 @@
             device_id_type=MESH,
         )
 
-    every_group = all_of(mass_group.at[1:], group_send, group_recv)
-    every_group.wait_recv()
-    total = jnp.zeros(mass_group.shape[1:], jnp.float32)
-    for a in range(group):
-        total = total + mass_group[lax.rem(rank - a + group, group)]
-    mass_line[0] = total
-
+    every_line = all_of(mass_line.at[1:], line_send, line_recv)
     beyond = size_y - 1 - iy + up.astype(jnp.int32) + turn_before.astype(jnp.int32)
 
-    @pl.when(beyond > 0)
+    def to_line():
+        for k in range(2, bits + 1):
+            mass_join(k)
+            if k < bits:
+                meet(k)
+                mass_copy(k + 1).start()
+        mass_line[0] = mass_own[bits + 1]
+
+        @pl.when(beyond > 0)
+        def _():
+            pl.semaphore_wait(far_ready, beyond)
+
+        for k in range(1, size_y):
+            pltpu.make_async_remote_copy(
+                src_ref=mass_line.at[0],
+                dst_ref=mass_line.at[k],
+                send_sem=line_send,
+                recv_sem=line_recv,
+                device_id=(ix, lax.rem(iy + k, size_y), iz),
+                device_id_type=MESH,
+            ).start()
+
+    late = [step for step in steps if step[0] == 0 and step[3] is None]
+    first = [step for step in steps if step[0] == 0 and step[3] is not None]
+
+    meet(orders[1][0])
+
+    @pl.when(jnp.logical_not(leads))
     def _():
-        pl.semaphore_wait(far_ready, beyond)
-
-    for k in range(1, size_y):
-        pltpu.make_async_remote_copy(
-            src_ref=mass_line.at[0],
-            dst_ref=mass_line.at[k],
-            send_sem=line_send,
-            recv_sem=line_recv,
-            device_id=(ix, lax.rem(iy + k, size_y), iz),
-            device_id_type=MESH,
-        ).start()
-    every_line = all_of(mass_line.at[1:], line_send, line_recv)
-
-    used = 6 * fields
+        mass_first()
+        pl.semaphore_wait(turn, 1)
+
+    for n, step in enumerate(first):
+        if n == 2:
+            pl.when(leads)(mass_first)
+        prepare(step[2], step[3])
+        to_chip(step).start()
+
+    def pass_turn(at):
+        if at not in (TURN_AT, TURN_LAST):
+            return
+        mine_now = leads
+        if TURN_AT != TURN_LAST:
+            mine_now = leads & (last_y if at == TURN_LAST else jnp.logical_not(last_y))
+
+        @pl.when(mine_now)
+        def _():
+            signal(turn, partner)
+
+    pass_turn(0)
+
+    for step in late:
+        for t in range(n_new):
+            prepare(step[2], t)
+
+    pass_turn(1)
+
+    if EARLY_X1:
+
+        @pl.when(leads)
+        def _():
+            for step in late:
+                to_chip(step).start()
+
+    mass_join(1)
+    if bits > 1:
+        meet(1)
+        mass_copy(2).start()
+
+    if not EARLY_X1:
+
+        @pl.when(leads)
+        def _():
+            for step in late:
+                to_chip(step).start()
+
+    pass_turn(2)
+
+    for step in steps:
+        j, c, x, s = step
+        if not j:
+            continue
+        meet(orders[c][j])
+        for t in range(n_new) if s is None else [s]:
+            prepare(x, t)
+            mine[x, c, t] = take(c, x, t, j)
+        if late:
+
+            @pl.when(jnp.logical_not(leads))
+            def _():
+                for other in late:
+                    to_chip(other).start()
+
+            late = []
+        to_chip(step).start()
+
+    for s in range(n_new):
+        prepare(0, s)
+
+    to_line()
+
     tall = faces.shape[1]
-    f_row = iota((tall, 2 * rows), 0)
-    f_col = iota((tall, 2 * rows), 1)
-    f_col = jnp.where(f_col >= rows, f_col - rows, f_col)
-    picks = (lax.div(f_row, 6) == lax.div(f_col, edge)) & (f_row < used)
-    f_x = lax.rem(f_col, edge)
-    gather = jnp.where(picks, 1.0, 0.0).astype(jnp.bfloat16)
-    ends = [
-        jnp.where(picks & (f_x == at), 1.0, 0.0).astype(jnp.bfloat16) for at in (0, edge - 1)
-    ]
-    u_row = iota((2 * rows, face), 0)
-    u_col = iota((2 * rows, face), 1)
-    diagonal = lax.rem(u_row, edge) == lax.div(u_col, edge)
-    diagonal = jnp.concatenate([diagonal] * 4, axis=1)
+    lane = iota((half, half * edge), 1)
+    place = lax.div(lane, edge) == iota((half, half * edge), 0)
+    along = lax.rem(lane, edge)
+    spot_z = lax.rem(lane, half) * edge
+    lower = along < half
     which = lax.rem(iota((tall, face), 0), 6)
+
+    def pick(tile, spot):
+        return jnp.take_along_axis(tile, spot, axis=1, mode="promise_in_bounds")
+
+    def layers(block):
+        left, right = block[:, : half * edge], block[:, half * edge :]
+        found = [pick(left, along), pick(right, along + (half - 1) * edge)]
+        for spot in (spot_z, spot_z + edge - 1):
+            found.append(jnp.where(lower, pick(left, spot), pick(right, spot)))
+        return [
+            jnp.sum(jnp.where(place, one, 0.0), axis=0, keepdims=True) for one in found
+        ]
 
     def face_copy(way, s):
         from_at, to_at = pl.ds(n_new, n_new), pl.ds(0 if way else 2 * n_new, n_new)
@@ -473,20 +583,17 @@
             total = take(c, 0, s, bits)
             for f in range(fields):
                 new_out[s, f, c * half : (c + 1) * half, :] = total[f]
-        high, low = split_two(new_out[s].reshape(rows, face))
-        both = jnp.concatenate([high, low], axis=0)
-        wide = dot(both, spread[...])
-        wide = jnp.where(diagonal, wide, 0.0).astype(jnp.bfloat16)
-        sides = dot(gather, wide)
-        layers = [dot(ends[0], both), dot(ends[1], both)]
-        layers += [sides[:, i * face : (i + 1) * face] for i in range(4)]
-        own = layers[0]
-        swapped = layers[1]
-        for e in range(1, 6):
-            own = jnp.where(which == e, layers[e], own)
-            swapped = jnp.where(which == e, layers[e ^ 1], swapped)
-        faces[s] = own
-        ghosts[n_new + s] = swapped
+        rows_of = []
+        for f in range(fields):
+            ends = [new_out[s, f, 0:1, :], new_out[s, f, edge - 1 : edge, :]]
+            parts_of = [
+                layers(new_out[s, f, c * half : (c + 1) * half, :]) for c in range(2)
+            ]
+            sides = [jnp.concatenate(pair, axis=1) for pair in zip(*parts_of)]
+            rows_of.append(ends + sides)
+            for e in range(6):
+                at = 6 * f + e
+                ghosts[n_new + s, at : at + 1, :] = rows_of[f][e ^ 1]
 
         @pl.when(has_after)
         def _(s=s):
@@ -496,8 +603,13 @@
         def _(s=s):
             face_copy(0, s).start()
 
+        for f in range(fields):
+            for e in range(6):
+                at = 6 * f + e
+                faces[s, at : at + 1, :] = rows_of[f][e]
+
     every_line.wait_recv()
-    total = jnp.zeros(mass_group.shape[1:], jnp.float32)
+    total = jnp.zeros(mass_line.shape[1:], jnp.float32)
     for a in range(size_y):
         total = total + mass_line[lax.rem(iy - a + size_y, size_y)]
     total = total / float(n_old * devices * edge * face)
@@ -506,7 +618,8 @@
 
     all_of(theirs, d2d_send, d2d_recv.at[0]).wait_send()
     all_of(chip_in, chip_send, chip_recv.at[0]).wait_send()
-    every_group.wait_send()
+    for k in range(bits + 1):
+        mass_copy(k).wait_send()
     every_line.wait_send()
 
     @pl.when(has_before)
@@ -550,8 +663,7 @@
     n_pairs = pair_old.shape[0]
     n_new = neighbor_side.shape[0]
     size_x, size_y, size_z = (lax.axis_size(a) for a in AXES)
-    group = size_x * size_z
-    chips = group // 2
+    chips = size_x * size_z // 2
     assert size_z % 2 == 0 and chips & (chips - 1) == 0
     half = edge // 2
     bits = chips.bit_length() - 1
@@ -570,21 +682,23 @@
         out_specs=(vmem, vmem, vmem),
         scratch_shapes=[pltpu.SMEM(t.shape, jnp.int32) for t in tables]
         + [
+            pltpu.VMEM((2, face, face), jnp.int32),
+            pltpu.VMEM((2, fields * edge, 2 * fields * edge), jnp.int32),
             pltpu.VMEM((n_old, fields, edge, face), f32),
             pltpu.VMEM((n_pairs + 1, 2, fields, half, face), f32),
             pltpu.VMEM((chips, 2, n_new, fields, half, face), f32),
             pltpu.VMEM((chips, 2, n_new, fields, half, face), f32),
             pltpu.VMEM((chips, 2, n_new, fields, half, face), f32),
             pltpu.VMEM((chips - 1, 2, n_new, fields, half, face), f32),
-            pltpu.VMEM((face, 4 * face), jnp.bfloat16),
             pltpu.VMEM((n_new, tall, face), f32),
             pltpu.VMEM((3 * n_new, tall, face), f32),
-            pltpu.VMEM((group, 1, 128), f32),
+            pltpu.VMEM((bits + 2, 1, 128), f32),
+            pltpu.VMEM((bits + 1, 1, 128), f32),
             pltpu.VMEM((size_y, 1, 128), f32),
             dma,
             dma((len(tables),)),
             pltpu.SemaphoreType.REGULAR,
-            pltpu.SemaphoreType.REGULAR,
+            pltpu.SemaphoreType.REGULAR((bits,)),
             pltpu.SemaphoreType.REGULAR,
             dma,
             dma((n_new + chips - 1,)),
@@ -592,8 +706,8 @@
             dma((len(plan_of(bits, n_new)[1]),)),
             dma((2,)),
             dma((2,)),
-            dma,
-            dma,
+            dma((bits + 1,)),
+            dma((bits + 1,)),
             dma,
             dma,
         ],

time: 20.9 us -> 20.5 us (0.981)
  Pallas kernels: 20.1 us -> 19.7 us
    pallas_call x1, Pallas kernels: 19.3 us -> 19 us  [body(): pl.pallas_call(functools.partial(kernel, dims), out_shape=tuple((pltpu.VM...]
where the time goes in v2:
time: 20.5 us; the launch traced here: 20.4 us
  Pallas kernels  19.7 us (96%)
  between operations  0.64 us (3%)
    pallas_call x1, Pallas kernels, body(): pl.pallas_call(functools.partial(kernel, dims), out_shape=tuple((pltpu.VM...  19 us
    pallas_call x1, Pallas kernels, body(): pl.pallas_call(write_out, out_shape=tuple((jax.ShapeDtypeStruct(s, f32) f...  0.76 us

profile of v2, /device:TPU:19, one launch (start us, length us, event | category | flops | bytes accessed | tf_op | source)
XLA Modules:
  0.0 20.4 jit_solution(10785060203459573300)
XLA Ops:
  0.6 19.0 %shard_map.103 = (f32[3,5,16,256]{3,2,1,0:T(8,128)S(1)}, f32[3,5,6,256]{3,2,1,0:T(8,128)S(1)}, f32[2,5]{1,0:T(2,128)S(1)}) custom-call(f32[12,5,16,256]{3,2,1,0:T(8,128)} %old_hbm.1, s32[8]{0:T(128)} %pair_old_hbm.1, s32[8]{0:T(128)} %pair_slot_hbm.1, s32[3,8]{1,0:T(4,128)} %bitcast.2, s32[8]{0:T(128)} %bitcast.3, s32[96]{0:T(128)} %new_ratio_hbm.1, ...), custom_call_target="tpu_custom_call" | custom-call | tf_op jit(solution)/shard_map/pallas_call | solution.py:678
  19.6 0.8 %shard_map.104 = (f32[3,5,16,256]{3,2,1,0:T(8,128)}, f32[3,5,6,256]{3,2,1,0:T(8,128)}, f32[2,5]{1,0:T(2,128)}) custom-call(f32[3,5,16,256]{3,2,1,0:T(8,128)S(1)} %get-tuple-element.6.refs_0_, f32[3,5,6,256]{3,2,1,0:T(8,128)S(1)} %get-tuple-element.7.refs_1_, f32[2,5]{1,0:T(2,128)S(1)} %get-tuple-element.8.refs_2_), custom_call_target="tpu_custom_call" | custom-call | tf_op jit(solution)/shard_map/pallas_call | solution.py:716

commit v3 on v2

--- a/solution.py
+++ b/solution.py
@@ -9,10 +9,6 @@
 
 MESH = pl.DeviceIdType.MESH
 AXES = ("gx", "gy", "gz")
-TURN_AT = 2
-TURN_LAST = 1
-EARLY_X1 = True
-LEAD_MODE = 1
 
 
 def split_two(value):
@@ -29,7 +25,7 @@
     return lax.broadcasted_iota(jnp.int32, shape, axis)
 
 
-def plan_of(bits, n_new):
+def plan_of(bits, n_new, fields):
     chips = 1 << bits
     orders = [list(range(bits)), list(reversed(range(bits)))]
 
@@ -39,13 +35,17 @@
         return sorted(xs, key=lambda x: -bin(x).count("1"))
 
     steps = []
+    whole, cut = (0, fields), fields // 4 * 4
+    pieces = [(0, cut), (cut, fields)] if 0 < cut < fields else [whole]
     for j in range(bits):
         for pair in zip(*(sends(order, j) for order in orders)):
             fine = j == bits - 1 or pair[0] == chips - 1
             for s in range(n_new) if fine else [None]:
-                for c in range(2):
-                    steps.append((j, c, pair[c], s))
-    return orders, steps
+                last = j == bits - 1 and s == n_new - 1
+                for r in pieces if last else [whole]:
+                    for c in range(2):
+                        steps.append((j, c, pair[c], s, r))
+    return orders, steps, [[whole]] * (n_new - 1) + [pieces]
 
 
 def kernel(
@@ -74,27 +74,23 @@
     parts,
     mine,
     theirs,
-    partner_in,
-    chip_in,
+    inbox,
     faces,
     ghosts,
     mass_own,
     mass_in,
-    mass_line,
     old_sem,
     table_sem,
     turn,
     near,
     far_ready,
-    d2d_send,
+    bulk_send,
     d2d_recv,
-    chip_send,
     chip_recv,
     face_send,
     face_recv,
     mass_send,
     mass_recv,
-    line_send,
     line_recv,
 ):
     size_x, size_y, size_z, n_old, n_new, n_pairs, fields, edge = dims
@@ -256,12 +252,6 @@
 
     parts[n_pairs] = jnp.zeros(parts.shape[1:], jnp.float32)
     old_copy.wait()
-
-    old_acc = [jnp.zeros((8, face), jnp.float32) for _ in range(fields)]
-    for o in range(n_old):
-        for f in range(fields):
-            for h in range(edge // 8):
-                old_acc[f] = old_acc[f] + old[o, f, h * 8 : (h + 1) * 8, :]
 
     new_acc = [jnp.zeros((8, face), jnp.float32) for _ in range(fields)]
     for p in range(n_pairs):
@@ -301,13 +291,13 @@
             first = jnp.where(hit, jnp.int32(p), first)
         dst[x, :, s] = parts[first] + parts[second]
 
-    orders, steps = plan_of(bits, n_new)
+    orders, steps, pieces = plan_of(bits, n_new, fields)
 
     def d2d_key(x, s):
         return (x, s) if x == chips - 1 else (x, None)
 
     d2d_order = []
-    for _, _, x, s in steps:
+    for _, _, x, s, _ in steps:
         for t in range(n_new) if s is None else [s]:
             if d2d_key(x, t) not in d2d_order:
                 d2d_order.append(d2d_key(x, t))
@@ -318,8 +308,8 @@
         at = (x, slice(None), s) if s is not None else (x,)
         return pltpu.make_async_remote_copy(
             src_ref=theirs.at[at],
-            dst_ref=partner_in.at[at],
-            send_sem=d2d_send,
+            dst_ref=inbox.at[at],
+            send_sem=bulk_send,
             recv_sem=d2d_recv.at[d2d_order.index(key)],
             device_id=partner,
             device_id_type=MESH,
@@ -333,6 +323,12 @@
 
     send_theirs(d2d_order[:n_new])
 
+    old_acc = [jnp.zeros((8, face), jnp.float32) for _ in range(fields)]
+    for o in range(n_old):
+        for f in range(fields):
+            for h in range(edge // 8):
+                old_acc[f] = old_acc[f] + old[o, f, h * 8 : (h + 1) * 8, :]
+
     m_row = iota((16, 128), 0)
     m_col = iota((16, 128), 1)
     zero_rows = jnp.zeros((8 - fields, 128), jnp.float32)
@@ -352,7 +348,7 @@
         return pltpu.make_async_remote_copy(
             src_ref=mass_own.at[k],
             dst_ref=mass_in.at[k],
-            send_sem=mass_send.at[k],
+            send_sem=mass_send,
             recv_sem=mass_recv.at[k],
             device_id=near_chip(k - 1) if k else partner,
             device_id_type=MESH,
@@ -379,16 +375,17 @@
             to_partner(key).wait_recv()
         if (x, s) not in joined:
             joined.add((x, s))
-            mine[x, :, s] = mine[x, :, s] + partner_in[x, :, s]
+            mine[x, :, s] = mine[x, :, s] + inbox[x, :, s]
 
     def to_chip(step):
-        j, c, x, s = step
-        here = (x, c) if s is None else (x, c, s)
-        there = (x - 1, c) if s is None else (x - 1, c, s)
+        j, c, x, s, r = step
+        cut = () if s is None else (s,) if r == (0, fields) else (s, slice(*r))
+        here = (x, c) + cut
+        there = (chips + x - 1, c) + cut
         return pltpu.make_async_remote_copy(
             src_ref=mine.at[here],
-            dst_ref=chip_in.at[there],
-            send_sem=chip_send,
+            dst_ref=inbox.at[there],
+            send_sem=bulk_send,
             recv_sem=chip_recv.at[steps.index(step)],
             device_id=at_rank(chip_at(1 << orders[c][j]) * 2 + core),
             device_id_type=MESH,
@@ -396,22 +393,22 @@
 
     waited = set()
 
-    def take(c, x, s, j):
-        total = mine[x, c, s]
+    def take(c, x, s, j, r):
+        total = mine[x, c, s, r[0] : r[1]]
         for b in orders[c][:j]:
             y = x | (1 << b)
-            step = next(t for t in steps if t[1:3] == (c, y) and t[3] in (None, s))
+            step = next(
+                t
+                for t in steps
+                if t[1:3] == (c, y) and t[3] in (None, s) and t[4] in ((0, fields), r)
+            )
             if step not in waited:
                 waited.add(step)
                 to_chip(step).wait_recv()
-            total = total + chip_in[y - 1, c, s]
+            total = total + inbox[chips + y - 1, c, s, r[0] : r[1]]
         return total
 
-    leads = (core == 0) == (2 * iy < size_y)
-    if LEAD_MODE == 1:
-        leads = (core == 0) == (iy < size_y - 1)
-    if LEAD_MODE == 2:
-        leads = core == 0
+    leads = (core == 0) == (iy < size_y - 1)
     prepare(steps[0][2], 0)
 
     met = set()
@@ -440,7 +437,8 @@
             device_id_type=MESH,
         )
 
-    every_line = all_of(mass_line.at[1:], line_send, line_recv)
+    first_line = bits + 1
+    every_line = all_of(mass_in.at[first_line + 1 :], mass_send, line_recv)
     beyond = size_y - 1 - iy + up.astype(jnp.int32) + turn_before.astype(jnp.int32)
 
     def to_line():
@@ -449,7 +447,7 @@
             if k < bits:
                 meet(k)
                 mass_copy(k + 1).start()
-        mass_line[0] = mass_own[bits + 1]
+        mass_in[first_line] = mass_own[bits + 1]
 
         @pl.when(beyond > 0)
         def _():
@@ -457,9 +455,9 @@
 
         for k in range(1, size_y):
             pltpu.make_async_remote_copy(
-                src_ref=mass_line.at[0],
-                dst_ref=mass_line.at[k],
-                send_sem=line_send,
+                src_ref=mass_in.at[first_line],
+                dst_ref=mass_in.at[first_line + k],
+                send_sem=mass_send,
                 recv_sem=line_recv,
                 device_id=(ix, lax.rem(iy + k, size_y), iz),
                 device_id_type=MESH,
@@ -481,54 +479,42 @@
         prepare(step[2], step[3])
         to_chip(step).start()
 
-    def pass_turn(at):
-        if at not in (TURN_AT, TURN_LAST):
-            return
-        mine_now = leads
-        if TURN_AT != TURN_LAST:
-            mine_now = leads & (last_y if at == TURN_LAST else jnp.logical_not(last_y))
-
-        @pl.when(mine_now)
+    def pass_turn(now):
+        @pl.when(leads & now)
         def _():
             signal(turn, partner)
 
-    pass_turn(0)
+    pass_turn(last_y)
 
     for step in late:
         for t in range(n_new):
             prepare(step[2], t)
 
-    pass_turn(1)
-
-    if EARLY_X1:
-
-        @pl.when(leads)
-        def _():
-            for step in late:
-                to_chip(step).start()
+    @pl.when(leads & jnp.logical_not(last_y))
+    def _():
+        for step in late:
+            to_chip(step).start()
 
     mass_join(1)
     if bits > 1:
         meet(1)
         mass_copy(2).start()
 
-    if not EARLY_X1:
-
-        @pl.when(leads)
-        def _():
-            for step in late:
-                to_chip(step).start()
-
-    pass_turn(2)
+    @pl.when(leads & last_y)
+    def _():
+        for step in late:
+            to_chip(step).start()
+
+    pass_turn(jnp.logical_not(last_y))
 
     for step in steps:
-        j, c, x, s = step
+        j, c, x, s, r = step
         if not j:
             continue
         meet(orders[c][j])
         for t in range(n_new) if s is None else [s]:
             prepare(x, t)
-            mine[x, c, t] = take(c, x, t, j)
+            mine[x, c, t, r[0] : r[1]] = take(c, x, t, j, r)
         if late:
 
             @pl.when(jnp.logical_not(leads))
@@ -564,63 +550,61 @@
             jnp.sum(jnp.where(place, one, 0.0), axis=0, keepdims=True) for one in found
         ]
 
-    def face_copy(way, s):
+    def face_copy(way, s, r=None):
+        rows_at = () if r is None else (pl.ds(6 * r[0], (6 * r[1] + 7) // 8 * 8 - 6 * r[0]),)
         from_at, to_at = pl.ds(n_new, n_new), pl.ds(0 if way else 2 * n_new, n_new)
         if s is not None:
             from_at, to_at = n_new + s, s if way else 2 * n_new + s
         return pltpu.make_async_remote_copy(
-            src_ref=ghosts.at[from_at],
-            dst_ref=ghosts.at[to_at],
+            src_ref=ghosts.at[(from_at,) + rows_at],
+            dst_ref=ghosts.at[(to_at,) + rows_at],
             send_sem=face_send.at[way],
             recv_sem=face_recv.at[way],
             device_id=at_linear(linear + 1 if way else linear - 1),
             device_id_type=MESH,
         )
 
-
     for s in range(n_new):
-        for c in range(2):
-            total = take(c, 0, s, bits)
-            for f in range(fields):
-                new_out[s, f, c * half : (c + 1) * half, :] = total[f]
-        rows_of = []
-        for f in range(fields):
-            ends = [new_out[s, f, 0:1, :], new_out[s, f, edge - 1 : edge, :]]
-            parts_of = [
-                layers(new_out[s, f, c * half : (c + 1) * half, :]) for c in range(2)
-            ]
-            sides = [jnp.concatenate(pair, axis=1) for pair in zip(*parts_of)]
-            rows_of.append(ends + sides)
-            for e in range(6):
-                at = 6 * f + e
-                ghosts[n_new + s, at : at + 1, :] = rows_of[f][e ^ 1]
-
-        @pl.when(has_after)
-        def _(s=s):
-            face_copy(1, s).start()
-
-        @pl.when(has_before)
-        def _(s=s):
-            face_copy(0, s).start()
-
-        for f in range(fields):
-            for e in range(6):
-                at = 6 * f + e
-                faces[s, at : at + 1, :] = rows_of[f][e]
+        for r in pieces[s]:
+            for c in range(2):
+                total = take(c, 0, s, bits, r)
+                for f in range(*r):
+                    new_out[s, f, c * half : (c + 1) * half, :] = total[f - r[0]]
+            rows_of = {}
+            for f in range(*r):
+                ends = [new_out[s, f, 0:1, :], new_out[s, f, edge - 1 : edge, :]]
+                parts_of = [
+                    layers(new_out[s, f, c * half : (c + 1) * half, :]) for c in range(2)
+                ]
+                sides = [jnp.concatenate(pair, axis=1) for pair in zip(*parts_of)]
+                rows_of[f] = ends + sides
+                for e in range(6):
+                    at = 6 * f + e
+                    ghosts[n_new + s, at : at + 1, :] = rows_of[f][e ^ 1]
+
+            @pl.when(has_after)
+            def _(s=s, r=r):
+                face_copy(1, s, r).start()
+
+            @pl.when(has_before)
+            def _(s=s, r=r):
+                face_copy(0, s, r).start()
+
+            for f in range(*r):
+                for e in range(6):
+                    at = 6 * f + e
+                    faces[s, at : at + 1, :] = rows_of[f][e]
 
     every_line.wait_recv()
-    total = jnp.zeros(mass_line.shape[1:], jnp.float32)
+    total = jnp.zeros(mass_in.shape[1:], jnp.float32)
     for a in range(size_y):
-        total = total + mass_line[lax.rem(iy - a + size_y, size_y)]
+        total = total + mass_in[first_line + lax.rem(iy - a + size_y, size_y)]
     total = total / float(n_old * devices * edge * face)
     for a in range(2):
         mass_out[a : a + 1, :] = total[:, 8 * a : 8 * a + fields]
 
-    all_of(theirs, d2d_send, d2d_recv.at[0]).wait_send()
-    all_of(chip_in, chip_send, chip_recv.at[0]).wait_send()
-    for k in range(bits + 1):
-        mass_copy(k).wait_send()
-    every_line.wait_send()
+    all_of(inbox, bulk_send, chip_recv.at[0]).wait_send()
+    all_of(mass_in.at[: bits + size_y], mass_send, line_recv).wait_send()
 
     @pl.when(has_before)
     def _():
@@ -688,13 +672,11 @@
             pltpu.VMEM((n_pairs + 1, 2, fields, half, face), f32),
             pltpu.VMEM((chips, 2, n_new, fields, half, face), f32),
             pltpu.VMEM((chips, 2, n_new, fields, half, face), f32),
-            pltpu.VMEM((chips, 2, n_new, fields, half, face), f32),
-            pltpu.VMEM((chips - 1, 2, n_new, fields, half, face), f32),
+            pltpu.VMEM((2 * chips - 1, 2, n_new, fields, half, face), f32),
             pltpu.VMEM((n_new, tall, face), f32),
             pltpu.VMEM((3 * n_new, tall, face), f32),
             pltpu.VMEM((bits + 2, 1, 128), f32),
-            pltpu.VMEM((bits + 1, 1, 128), f32),
-            pltpu.VMEM((size_y, 1, 128), f32),
+            pltpu.VMEM((bits + 1 + size_y, 1, 128), f32),
             dma,
             dma((len(tables),)),
             pltpu.SemaphoreType.REGULAR,
@@ -702,13 +684,11 @@
             pltpu.SemaphoreType.REGULAR,
             dma,
             dma((n_new + chips - 1,)),
-            dma,
-            dma((len(plan_of(bits, n_new)[1]),)),
+            dma((len(plan_of(bits, n_new, fields)[1]),)),
             dma((2,)),
             dma((2,)),
+            dma,
             dma((bits + 1,)),
-            dma((bits + 1,)),
-            dma,
             dma,
         ],
         compiler_params=pltpu.CompilerParams(collective_id=0, has_side_effects=True),

time: 20.5 us -> 20.4 us (level)
  no operation moved by 1% of the time
where the time goes in v3:
time: 20.4 us; the launch traced here: 20.2 us
  Pallas kernels  19.6 us (96%)
  between operations  0.64 us (3%)
    pallas_call x1, Pallas kernels, body(): pl.pallas_call(functools.partial(kernel, dims), out_shape=tuple((pltpu.VM...  18.8 us
    pallas_call x1, Pallas kernels, body(): pl.pallas_call(write_out, out_shape=tuple((jax.ShapeDtypeStruct(s, f32) f...  0.76 us

profile of v3, /device:TPU:19, one launch (start us, length us, event | category | flops | bytes accessed | tf_op | source)
XLA Modules:
  0.0 20.2 jit_solution(12337909339274355645)
XLA Ops:
  0.6 18.8 %shard_map.103 = (f32[3,5,16,256]{3,2,1,0:T(8,128)S(1)}, f32[3,5,6,256]{3,2,1,0:T(8,128)S(1)}, f32[2,5]{1,0:T(2,128)S(1)}) custom-call(f32[12,5,16,256]{3,2,1,0:T(8,128)} %old_hbm.1, s32[8]{0:T(128)} %pair_old_hbm.1, s32[8]{0:T(128)} %pair_slot_hbm.1, s32[3,8]{1,0:T(4,128)} %bitcast.2, s32[8]{0:T(128)} %bitcast.3, s32[96]{0:T(128)} %new_ratio_hbm.1, ...), custom_call_target="tpu_custom_call" | custom-call | tf_op jit(solution)/shard_map/pallas_call | solution.py:662
  19.5 0.8 %shard_map.104 = (f32[3,5,16,256]{3,2,1,0:T(8,128)}, f32[3,5,6,256]{3,2,1,0:T(8,128)}, f32[2,5]{1,0:T(2,128)}) custom-call(f32[3,5,16,256]{3,2,1,0:T(8,128)S(1)} %get-tuple-element.6.refs_0_, f32[3,5,6,256]{3,2,1,0:T(8,128)S(1)} %get-tuple-element.7.refs_1_, f32[2,5]{1,0:T(2,128)S(1)} %get-tuple-element.8.refs_2_), custom_call_target="tpu_custom_call" | custom-call | tf_op jit(solution)/shard_map/pallas_call | solution.py:696

commit v4 on v3

--- a/solution.py
+++ b/solution.py
@@ -484,13 +484,13 @@
         def _():
             signal(turn, partner)
 
-    pass_turn(last_y)
-
     for step in late:
         for t in range(n_new):
             prepare(step[2], t)
 
-    @pl.when(leads & jnp.logical_not(last_y))
+    pass_turn(last_y)
+
+    @pl.when(leads)
     def _():
         for step in late:
             to_chip(step).start()
@@ -499,11 +499,6 @@
     if bits > 1:
         meet(1)
         mass_copy(2).start()
-
-    @pl.when(leads & last_y)
-    def _():
-        for step in late:
-            to_chip(step).start()
 
     pass_turn(jnp.logical_not(last_y))
 

time: 20.4 us -> 20.4 us (level)
  no operation moved by 1% of the time
where the time goes in v4:
time: 20.4 us; the launch traced here: 20.2 us
  Pallas kernels  19.6 us (96%)
  between operations  0.64 us (3%)
    pallas_call x1, Pallas kernels, body(): pl.pallas_call(functools.partial(kernel, dims), out_shape=tuple((pltpu.VM...  18.8 us
    pallas_call x1, Pallas kernels, body(): pl.pallas_call(write_out, out_shape=tuple((jax.ShapeDtypeStruct(s, f32) f...  0.76 us

profile of v4, /device:TPU:19, one launch (start us, length us, event | category | flops | bytes accessed | tf_op | source)
XLA Modules:
  0.0 20.2 jit_solution(18060800922058999148)
XLA Ops:
  0.6 18.8 %shard_map.103 = (f32[3,5,16,256]{3,2,1,0:T(8,128)S(1)}, f32[3,5,6,256]{3,2,1,0:T(8,128)S(1)}, f32[2,5]{1,0:T(2,128)S(1)}) custom-call(f32[12,5,16,256]{3,2,1,0:T(8,128)} %old_hbm.1, s32[8]{0:T(128)} %pair_old_hbm.1, s32[8]{0:T(128)} %pair_slot_hbm.1, s32[3,8]{1,0:T(4,128)} %bitcast.2, s32[8]{0:T(128)} %bitcast.3, s32[96]{0:T(128)} %new_ratio_hbm.1, ...), custom_call_target="tpu_custom_call" | custom-call | tf_op jit(solution)/shard_map/pallas_call | solution.py:657
  19.5 0.8 %shard_map.104 = (f32[3,5,16,256]{3,2,1,0:T(8,128)}, f32[3,5,6,256]{3,2,1,0:T(8,128)}, f32[2,5]{1,0:T(2,128)}) custom-call(f32[3,5,16,256]{3,2,1,0:T(8,128)S(1)} %get-tuple-element.6.refs_0_, f32[3,5,6,256]{3,2,1,0:T(8,128)S(1)} %get-tuple-element.7.refs_1_, f32[2,5]{1,0:T(2,128)S(1)} %get-tuple-element.8.refs_2_), custom_call_target="tpu_custom_call" | custom-call | tf_op jit(solution)/shard_map/pallas_call | solution.py:691
